TPU v7x, 32 devices: a whole 2x2x4 slice. The times are simulated.
32 devices in a mesh: robot: 8 (over z, x), sub: 4 (over y, core).
Axes of the slice: x: 2, y: 2, z: 4, core: 2. Of those that a mesh axis runs over, the one named last changes fastest.
Arguments:
- landmark_copies: float32 [8, 4, 3, 512], P('robot', 'sub'), may hold values from -6 to 6
- dual_copies: float32 [8, 4, 3, 512], P('robot', 'sub'), may hold values from -4 to 4
- visibility: int32 [8, 4, 512], P('robot', 'sub'), may hold values from 0 to 511
- block_counts: int32 [8, 4, 8], P('robot', 'sub'), may hold values from 1 to 64, as said below
- consensus_old: float32 [8, 4, 3, 512], P('robot', 'sub'), may hold values from -6 to 6
- poses: float32 [8, 4, 6, 1024], P('robot', 'sub'), may hold values from -6 to 6
- inverse_blocks: float32 [8, 4, 36, 1024], P('robot', 'sub'), may hold values from -1.8 to 1.8
- jacobians: float32 [8, 4, 18, 4096], P('robot', 'sub'), may hold values from -3 to 3
- measurements: float32 [8, 4, 3, 4096], P('robot', 'sub'), may hold values from -6 to 6
- obs_pose: int32 [8, 4, 4096], P('robot', 'sub'), may hold values from 0 to 1023
- obs_slot: int32 [8, 4, 4096], P('robot', 'sub'), may hold values from 0 to 511, as said below
- edge_to: int32 [8, 4, 1024], P('robot', 'sub'), may hold values from 0 to 4095
- edge_offset: float32 [8, 4, 6, 1024], P('robot', 'sub'), may hold values from -3 to 3
Outputs:
- refined_poses: float32 [8, 4, 6, 1024], P('robot', 'sub')
- consensus: float32 [8, 4, 3, 512], P('robot', 'sub')
- dual_new: float32 [8, 4, 3, 512], P('robot', 'sub')
- residual_norms: float32 [2], replicated
Inputs may be any that keep to these rules, and one draw needn't show every extreme that they name: block_counts[r,s,d] counts the live slots at the head of block d; for every sub index some robot receives full blocks from every robot, which robot varies with the draw. `obs_slot`: each observation names a live slot of its own device.
All inputs are finite; a program needn't handle non-finite values.
Results may differ from a plain program's by a relative error of at most 0.0001.
Values sent between devices are 32-bit elements; how exact they have to be, the bound alone decides.
No kernel may reach another device: no remote copies, remote signals or barrier semaphores. Data moves between devices by JAX's collectives and lax.ppermute only.
A program may use at most 64 MiB of HBM per device.

v0:
```python
import jax
import jax.numpy as jnp
from jax import lax
from jax.sharding import PartitionSpec as P

penalty = 2.0


def body(
    landmark_copies,
    dual_copies,
    visibility,
    block_counts,
    consensus_old,
    poses,
    inverse_blocks,
    jacobians,
    measurements,
    obs_pose,
    obs_slot,
    edge_to,
    edge_offset,
):
    copies = landmark_copies[0, 0]
    duals = dual_copies[0, 0]
    slot_ids = visibility[0]
    counts = block_counts[0, 0]
    old_estimate = consensus_old[0, 0]
    robots = lax.axis_size("robot")
    slot_count = copies.shape[1]
    block_size = slot_count // robots
    owned = old_estimate.shape[1]
    live_mask = (
        (jnp.arange(block_size)[None, :] < counts[:, None]).reshape(slot_count).astype(jnp.float32)
    )
    outgoing = jnp.concatenate([(copies + duals) * live_mask[None, :], live_mask[None, :]], axis=0)
    received, received_ids = (
        lax.all_to_all(outgoing, "robot", split_axis=1, concat_axis=1, tiled=True),
        lax.all_to_all(slot_ids, "robot", split_axis=1, concat_axis=1, tiled=True),
    )
    owner_ids = received_ids[0]
    totals = jax.vmap(lambda entries: jax.ops.segment_sum(entries, owner_ids, num_segments=owned))(
        received
    )
    consensus = (old_estimate + totals[:3]) / (1.0 + totals[3:4])
    returning = consensus[:, owner_ids]
    back = lax.all_to_all(returning, "robot", split_axis=1, concat_axis=1, tiled=True)
    differ = (copies - back) * live_mask[None, :]
    dual_new = duals + differ
    primal = jnp.sum(differ * differ)
    change = consensus - old_estimate
    dualsum = penalty * penalty * jnp.sum(totals[3:4] * change * change)
    primal_all, dual_all = lax.psum((primal, dualsum), ("robot", "sub"))
    landmark_total = owned * robots * lax.axis_size("sub")
    residual_norms = jnp.sqrt(jnp.stack([primal_all, dual_all]) / landmark_total)
    pose_block = poses[0, 0]
    pose_count = pose_block.shape[1]
    robot_all = lax.all_gather(pose_block, "sub", axis=1, tiled=True)
    pose_far = robot_all[:, edge_to[0, 0]]
    copies_at = copies[:, obs_slot[0, 0]]
    error = measurements[0, 0] - copies_at
    jac_rows = jacobians[0, 0].reshape(3, 6, error.shape[1])
    pull = jnp.sum(jac_rows * error[:, None, :], axis=0)
    pose_ids = obs_pose[0, 0]
    grad_obs = jax.vmap(
        lambda entries: jax.ops.segment_sum(entries, pose_ids, num_segments=pose_count)
    )(pull)
    grad = grad_obs + pose_far - pose_block - edge_offset[0, 0]
    inverse = inverse_blocks[0, 0].reshape(6, 6, pose_count)
    delta = jnp.sum(inverse * grad[None, :, :], axis=1)
    refined = pose_block + delta
    return (refined[None, None], consensus[None, None], dual_new[None, None], residual_norms)


def solution(mesh):
    return jax.shard_map(
        body,
        mesh=mesh,
        in_specs=(
            P("robot", "sub", None, None),
            P("robot", "sub", None, None),
            P("robot", "sub", None),
            P("robot", "sub", None),
            P("robot", "sub", None, None),
            P("robot", "sub", None, None),
            P("robot", "sub", None, None),
            P("robot", "sub", None, None),
            P("robot", "sub", None, None),
            P("robot", "sub", None),
            P("robot", "sub", None),
            P("robot", "sub", None),
            P("robot", "sub", None, None),
        ),
        out_specs=(
            P("robot", "sub", None, None),
            P("robot", "sub", None, None),
            P("robot", "sub", None, None),
            P(),
        ),
        check_vma=False,
    )
```

profile of v0, /device:TPU:0, one launch (start us, length us, event | category | flops | bytes accessed | tf_op | source)
XLA Modules:
  0.0 154.9 jit_solution(5562532823633209940)
XLA Ops:
  0.6 0.5 broadcast.115
  1.1 1.3 reduce.16
  2.5 0.7 all_to_all.22
  3.2 7.3 %all-to-all-start = ((s32[1,8,64]{2,0,1:T(1,128)}), s32[1,8,64]{2,0,1:T(1,128)S(1)}, u32[]{:S(2)}, u32[]{:S(2)}) async-start(s32[1,8,64]{2,0,1:T(1,128)} %all_to_all.22), calls=%async_computation | async-start | bytes 8192 | tf_op jit(solution)/shard_map/all_to_all | solution.py:39
  10.4 0.7 fusion.8
  11.2 0.7 fusion.9
  11.9 0.8 copy.53
  12.7 0.7 add_reduce_fusion.1
  13.5 0.1 add.79
  13.6 0.7 compare_select_fusion
  14.3 1.4 copy.52
  15.7 14.1 %gather_fusion.1 = f32[4096,3]{1,0:T(8,128)} fusion(f32[3,512]{0,1:T(8,128)S(1)} %bitcast.54, s32[4096]{0:T(1024)S(1)} %broadcast_clamp_fusion), kind=kCustom, calls=%fused_computation.1 | custom fusion | bytes 114688 | tf_op jit(solution)/shard_map/gather | solution.py:60
  29.8 3.2 %bitcast_subtract_fusion = f32[3,4096]{0,1:T(8,128)} fusion(f32[4096,3]{1,0:T(8,128)} %gather_fusion.1, f32[1,1,3,4096]{2,3,1,0:T(8,128)S(1)} %copy.52), kind=kLoop, calls=%fused_computation.5 | loop fusion | flops 12288 | bytes 147456 | tf_op jit(solution)/shard_map/sub | solution.py:61
  33.0 2.3 %copy.54 = f32[3,4096]{1,0:T(4,128)S(1)} copy(f32[3,4096]{0,1:T(8,128)} %bitcast_subtract_fusion) | data formatting | bytes 98304 | tf_op jit(solution)/shard_map/sub | solution.py:61
  35.2 0.0 copy-done.1
  35.2 0.7 reduce.1
  36.0 0.1 multiply_reduce_fusion
  36.1 2.0 %copy.55 = f32[4096,6]{1,0:T(8,128)} copy(f32[4096,6]{0,1:T(8,128)S(1)} %bitcast.57) | data formatting | bytes 196608 | tf_op jit(solution)/shard_map/reduce_sum | solution.py:63
  38.1 0.2 copy.51
  38.3 15.8 %all-gather = f32[1,1,6,4096]{2,3,1,0:T(8,128)S(1)} all-gather(f32[1,1,6,1024]{2,3,1,0:T(8,128)S(1)} %copy.51), channel_id=2, replica_groups=mesh['robot'=8,'sub'=4] {'sub'}, dimensions={3}, use_global_device_ids=true | all-gather | bytes 122880 | tf_op jit(solution)/shard_map/all_gather | solution.py:58
  54.1 1.0 copy.57
  55.1 2.8 %gather_fusion = f32[1024,6]{1,0:T(8,128)S(1)} fusion(f32[6,4096]{0,1:T(8,128)S(1)} %bitcast.55, s32[1024]{0:T(1024)S(1)} %broadcast_clamp_fusion.1), kind=kCustom, calls=%fused_computation | custom fusion | bytes 53248 | tf_op jit(solution)/shard_map/gather | solution.py:59
  58.0 0.0 copy-start.2
  58.0 22.9 %scatter_fusion = f32[6,1024]{0,1:T(8,128)S(1)} fusion(f32[6,1024]{0,1:T(8,128)S(1)} %bitcast.53, s32[4096]{0:T(1024)S(1)} %bitcast.67, f32[4096,6]{1,0:T(8,128)} %copy.55), kind=kCustom, calls=%fused_computation.3 | custom fusion | flops 24576 | bytes 311296 | tf_op jit(solution)/shard_map/vmap()/scatter-add | solution.py:66
  80.9 0.0 copy-done
  80.9 0.0 copy-start.8
  80.9 0.1 bitcast_subtract_fusion.1
  81.0 0.2 copy.58
  81.2 0.4 reduce
  81.6 0.0 copy-start.4
  81.6 0.0 copy-start.6
  81.6 0.1 multiply_reduce_fusion.1
  81.7 0.7 reshape.262
  82.4 0.1 copy.59
  82.6 0.0 all-to-all-done
  82.6 6.0 %all-to-all-start.1 = ((f32[8,1,256]{2,1,0:T(1,128)}), f32[8,1,256]{2,1,0:T(1,128)S(1)}, u32[]{:S(2)}, u32[]{:S(2)}) async-start(f32[8,1,256]{2,1,0:T(1,128)} %reshape.262), calls=%async_computation.1 | async-start | bytes 16384 | tf_op jit(solution)/shard_map/all_to_all | solution.py:38
  88.6 0.1 broadcast_in_dim_squeeze.8
  88.7 0.7 reduce.17
  89.3 0.1 reshape.227
  89.4 5.7 %all-to-all-done.1 = f32[8,1,256]{2,1,0:T(1,128)S(1)} async-done(((f32[8,1,256]{2,1,0:T(1,128)}), f32[8,1,256]{2,1,0:T(1,128)S(1)}, u32[]{:S(2)}, u32[]{:S(2)}) %all-to-all-start.1) | async-done | bytes 8224 | tf_op jit(solution)/shard_map/all_to_all | solution.py:38
  95.1 0.5 broadcast.117
  95.6 0.7 reduce.18
  96.3 0.1 reshape.263
  96.4 0.1 reshape.226
  96.5 0.1 copy.62
  96.6 2.3 %scatter_custom_fusion.1 = f32[4,512]{0,1:T(8,128)S(1)} fusion(s32[512]{0:T(512)S(1)} %reshape.227, f32[512,4]{1,0:T(8,128)S(1)} %copy.62, f32[]{:T(128)} %constant.10.clone.1), kind=kCustom, calls=%fused_computation.21 | custom fusion | flops 2048 | bytes 8196 | tf_op jit(solution)/shard_map/vmap()/scatter-add | solution.py:42
  98.9 0.3 slice_reduce_fusion
  99.2 0.8 fusion
  100.0 1.0 gather_fusion.2
  101.1 0.1 copy.63
  101.2 0.7 reshape.264
  101.9 3.3 %all-to-all-start.2 = ((f32[8,1,192]{2,1,0:T(1,128)}), f32[8,1,192]{2,1,0:T(1,128)S(1)}, u32[]{:S(2)}, u32[]{:S(2)}) async-start(f32[8,1,192]{2,1,0:T(1,128)} %reshape.264), calls=%async_computation.2 | async-start | bytes 16384 | tf_op jit(solution)/shard_map/all_to_all | solution.py:47
  105.3 0.6 reshape_add_fusion
  105.9 0.1 reshape.192
  106.0 0.7 copy.68
  107.3 4.4 %all-to-all-done.2 = f32[8,1,192]{2,1,0:T(1,128)S(1)} async-done(((f32[8,1,192]{2,1,0:T(1,128)}), f32[8,1,192]{2,1,0:T(1,128)S(1)}, u32[]{:S(2)}, u32[]{:S(2)}) %all-to-all-start.2) | async-done | bytes 6176 | tf_op jit(solution)/shard_map/all_to_all | solution.py:47
  111.7 0.7 reduce.19
  112.4 0.1 reshape.265
  112.5 0.2 copy.67
  112.6 0.1 all_to_all.28
  112.7 0.7 fusion.4
  113.5 0.6 copy.69
  114.1 38.9 %all-reduce = (f32[1]{0:T(128)}, f32[1]{0:T(128)}) all-reduce(f32[1]{0:T(128)} %bitcast.22, f32[1]{0:T(128)} %bitcast.21), channel_id=1, replica_groups=mesh['robot'=8,'sub'=4] {'robot','sub'}, use_global_device_ids=true, to_apply=%region_7.0 | all-reduce | flops 2 | bytes 16 | tf_op jit(solution)/shard_map/psum | solution.py:53
  153.0 1.9 %fusion.10 = f32[2]{0:T(128)} fusion(f32[1]{0:T(128)} %get-tuple-element.22, f32[1]{0:T(128)} %get-tuple-element.23), kind=kLoop, calls=%fused_computation.41 | loop fusion | flops 4 | bytes 16 | tf_op jit(solution)/shard_map/sqrt | solution.py:55
  (27 shorter events, 0.2 us)
Async XLA Ops:
  3.2 79.4 %all-to-all-start = ((s32[1,8,64]{2,0,1:T(1,128)}), s32[1,8,64]{2,0,1:T(1,128)S(1)}, u32[]{:S(2)}, u32[]{:S(2)}) async-start(s32[1,8,64]{2,0,1:T(1,128)} %all_to_all.22), calls=%async_computation | async-start | bytes 8192 | tf_op jit(solution)/shard_map/all_to_all | solution.py:39
  33.0 2.3 %copy-start.1 = (f32[1,1,18,4096]{3,1,2,0:T(1,128)S(1)}, f32[1,1,18,4096]{3,1,2,0:T(1,128)}, u32[]{:S(2)}) copy-start(f32[1,1,18,4096]{3,1,2,0:T(1,128)} %param.20) | copy-start | bytes 884740
  35.2 2.8 %copy-start.3 = (f32[1,1,6,1024]{3,1,2,0:T(1,128)S(1)}, f32[1,1,6,1024]{3,1,2,0:T(1,128)}, u32[]{:S(2)}) copy-start(f32[1,1,6,1024]{3,1,2,0:T(1,128)} %param.18) | copy-start | bytes 73732
  38.1 16.0 %copy-start.9 = (s32[1,1,1024]{2,1,0:T(1,128)S(1)}, s32[1,1,1024]{2,1,0:T(1,128)}, u32[]{:S(2)}) copy-start(s32[1,1,1024]{2,1,0:T(1,128)} %param.24) | copy-start | bytes 12292
  38.1 16.0 %copy-start.5 = (f32[1,1,6,1024]{3,1,2,0:T(1,128)S(1)}, f32[1,1,6,1024]{3,1,2,0:T(1,128)}, u32[]{:S(2)}) copy-start(f32[1,1,6,1024]{3,1,2,0:T(1,128)} %param.25) | copy-start | bytes 73732
  38.1 19.9 %copy-start.7 = (s32[1,1,4096]{2,1,0:T(1,128)S(1)}, s32[1,1,4096]{2,1,0:T(1,128)}, u32[]{:S(2)}) copy-start(s32[1,1,4096]{2,1,0:T(1,128)} %param.22) | copy-start | bytes 49156
  57.9 23.0 %copy-start = (f32[1,1,6,1024]{2,3,1,0:T(8,128)S(1)}, f32[1,1,6,1024]{2,3,1,0:T(8,128)}, u32[]{:S(2)}) copy-start(f32[1,1,6,1024]{2,3,1,0:T(8,128)} %copy.57) | copy-start | bytes 73732
  58.0 23.2 %copy-start.2 = (f32[1,1,36,1024]{3,1,2,0:T(1,128)S(1)}, f32[1,1,36,1024]{3,1,2,0:T(1,128)}, u32[]{:S(2)}) copy-start(f32[1,1,36,1024]{3,1,2,0:T(1,128)} %param.19) | copy-start | bytes 442372
  80.9 1.5 copy-start.8
  81.6 31.9 %copy-start.4 = (f32[1,1,3,512]{3,1,2,0:T(1,128)S(1)}, f32[1,1,3,512]{3,1,2,0:T(1,128)}, u32[]{:S(2)}) copy-start(f32[1,1,3,512]{3,1,2,0:T(1,128)} %param.13) | copy-start | bytes 18436
  81.6 31.9 %copy-start.6 = (f32[1,1,3,512]{3,1,2,0:T(1,128)S(1)}, f32[1,1,3,512]{3,1,2,0:T(1,128)}, u32[]{:S(2)}) copy-start(f32[1,1,3,512]{3,1,2,0:T(1,128)} %param.14) | copy-start | bytes 18436
  82.6 12.5 %all-to-all-start.1 = ((f32[8,1,256]{2,1,0:T(1,128)}), f32[8,1,256]{2,1,0:T(1,128)S(1)}, u32[]{:S(2)}, u32[]{:S(2)}) async-start(f32[8,1,256]{2,1,0:T(1,128)} %reshape.262), calls=%async_computation.1 | async-start | bytes 16384 | tf_op jit(solution)/shard_map/all_to_all | solution.py:38
  101.9 9.8 %all-to-all-start.2 = ((f32[8,1,192]{2,1,0:T(1,128)}), f32[8,1,192]{2,1,0:T(1,128)S(1)}, u32[]{:S(2)}, u32[]{:S(2)}) async-start(f32[8,1,192]{2,1,0:T(1,128)} %reshape.264), calls=%async_computation.2 | async-start | bytes 16384 | tf_op jit(solution)/shard_map/all_to_all | solution.py:47
where the time goes:
time: 156 us; the launch traced here: 155 us
  blocking collectives  54.7 us (35%)
  other arithmetic  40.4 us (26%)
  local copies, waits for them, and re-layouts  31.6 us (20%)
  starting transfers between devices  16.6 us (11%)
  waiting for transfers between devices  10.1 us (6%)
  between operations  1.6 us (1%)
    psum x1, blocking collectives, body(): primal_all, dual_all = lax.psum((primal, dualsum), ('robot', 'sub'))  38.9 us
    scatter-add x1, other arithmetic, body(): jax.ops.segment_sum(entries, pose_ids, num_segments=pose_count)  22.9 us
    all_gather x1, blocking collectives, body(): robot_all = lax.all_gather(pose_block, 'sub', axis=1, tiled=True)  15.8 us
    gather x1, local copies, waits for them, and re-layouts, body(): copies_at = copies[:, obs_slot[0, 0]]  14.1 us
    all_to_all x1, starting transfers between devices, body(): lax.all_to_all(slot_ids, 'robot', split_axis=1, concat_axis=1, tiled=True)  7.28 us
    unnamed x32, local copies, waits for them, and re-layouts  7.06 us
    all_to_all x1, starting transfers between devices, body(): lax.all_to_all(outgoing, 'robot', split_axis=1, concat_axis=1, tiled=True)  6.01 us
    all_to_all x1, waiting for transfers between devices, body(): lax.all_to_all(outgoing, 'robot', split_axis=1, concat_axis=1, tiled=True)  5.69 us
  transfers between devices with their start and end apart: 3, of which 2 were waited for; matrix products, arithmetic and copies ran while one was open for 38% of the time, Pallas kernels for 0%

commit v1 on v0

--- a/solution.py
+++ b/solution.py
@@ -50,7 +50,7 @@
     primal = jnp.sum(differ * differ)
     change = consensus - old_estimate
     dualsum = penalty * penalty * jnp.sum(totals[3:4] * change * change)
-    primal_all, dual_all = lax.psum((primal, dualsum), ("robot", "sub"))
+    primal_all, dual_all = lax.psum(lax.psum((primal, dualsum), "sub"), "robot")
     landmark_total = owned * robots * lax.axis_size("sub")
     residual_norms = jnp.sqrt(jnp.stack([primal_all, dual_all]) / landmark_total)
     pose_block = poses[0, 0]

time: 156 us -> 141 us (0.904)
  blocking collectives: 54.7 us -> 40.7 us
    psum x1 -> x2, blocking collectives: 38.9 us -> 24.9 us  [body(): primal_all, dual_all = lax.psum(lax.psum((primal, dualsum), 'sub'), 'robot')]
  transfers between devices with their start and end apart: 3 -> 3, of which waited for: 2 -> 2; matrix products, arithmetic and copies ran while one was open for 38% -> 41% of each run, Pallas kernels for 0% -> 0%
where the time goes in v1:
time: 141 us
  blocking collectives  40.7 us (29%)
  other arithmetic  40.2 us (29%)
  local copies, waits for them, and re-layouts  31.6 us (22%)
  starting transfers between devices  16.6 us (12%)
  waiting for transfers between devices  10.1 us (7%)
  between operations  1.6 us (1%)
    psum x2, blocking collectives, body(): primal_all, dual_all = lax.psum(lax.psum((primal, dualsum), 'sub'), 'robot')  24.9 us
    scatter-add x1, other arithmetic, body(): jax.ops.segment_sum(entries, pose_ids, num_segments=pose_count)  22.9 us
    all_gather x1, blocking collectives, body(): robot_all = lax.all_gather(pose_block, 'sub', axis=1, tiled=True)  15.8 us
    gather x1, local copies, waits for them, and re-layouts, body(): copies_at = copies[:, obs_slot[0, 0]]  14.1 us
    all_to_all x1, starting transfers between devices, body(): lax.all_to_all(slot_ids, 'robot', split_axis=1, concat_axis=1, tiled=True)  7.28 us
    unnamed x32, local copies, waits for them, and re-layouts  7.06 us
    all_to_all x1, starting transfers between devices, body(): lax.all_to_all(outgoing, 'robot', split_axis=1, concat_axis=1, tiled=True)  6.01 us
    all_to_all x1, waiting for transfers between devices, body(): lax.all_to_all(outgoing, 'robot', split_axis=1, concat_axis=1, tiled=True)  5.69 us
  transfers between devices with their start and end apart: 3, of which 2 were waited for; matrix products, arithmetic and copies ran while one was open for 41% of the time, Pallas kernels for 0%

profile of v1, /device:TPU:0, one launch (start us, length us, event | category | flops | bytes accessed | tf_op | source)
XLA Modules:
  0.0 140.8 jit_solution(10189685594831924668)
XLA Ops:
  0.6 0.5 broadcast.115
  1.1 1.3 reduce.16
  2.5 0.7 all_to_all.22
  3.2 7.3 %all-to-all-start = ((s32[1,8,64]{2,0,1:T(1,128)}), s32[1,8,64]{2,0,1:T(1,128)S(1)}, u32[]{:S(2)}, u32[]{:S(2)}) async-start(s32[1,8,64]{2,0,1:T(1,128)} %all_to_all.22), calls=%async_computation | async-start | bytes 8192 | tf_op jit(solution)/shard_map/all_to_all | solution.py:39
  10.4 0.7 fusion.8
  11.2 0.7 fusion.9
  11.9 0.8 copy.53
  12.7 0.7 add_reduce_fusion.1
  13.5 0.1 add.83
  13.6 0.7 compare_select_fusion
  14.3 1.4 %copy.52 = f32[1,1,3,4096]{2,3,1,0:T(8,128)S(1)} copy(f32[1,1,3,4096]{3,1,2,0:T(1,128)} %param.21) | data formatting | bytes 98304 | tf_op args[8]
  15.7 14.1 %gather_fusion.1 = f32[4096,3]{1,0:T(8,128)} fusion(f32[3,512]{0,1:T(8,128)S(1)} %bitcast.54, s32[4096]{0:T(1024)S(1)} %broadcast_clamp_fusion), kind=kCustom, calls=%fused_computation.1 | custom fusion | bytes 114688 | tf_op jit(solution)/shard_map/gather | solution.py:60
  29.8 3.2 %bitcast_subtract_fusion = f32[3,4096]{0,1:T(8,128)} fusion(f32[4096,3]{1,0:T(8,128)} %gather_fusion.1, f32[1,1,3,4096]{2,3,1,0:T(8,128)S(1)} %copy.52), kind=kLoop, calls=%fused_computation.5 | loop fusion | flops 12288 | bytes 147456 | tf_op jit(solution)/shard_map/sub | solution.py:61
  33.0 2.3 %copy.54 = f32[3,4096]{1,0:T(4,128)S(1)} copy(f32[3,4096]{0,1:T(8,128)} %bitcast_subtract_fusion) | data formatting | bytes 98304 | tf_op jit(solution)/shard_map/sub | solution.py:61
  35.2 0.0 copy-done.1
  35.2 0.7 reduce.1
  36.0 0.1 multiply_reduce_fusion
  36.1 2.0 %copy.55 = f32[4096,6]{1,0:T(8,128)} copy(f32[4096,6]{0,1:T(8,128)S(1)} %bitcast.57) | data formatting | bytes 196608 | tf_op jit(solution)/shard_map/reduce_sum | solution.py:63
  38.1 0.2 copy.51
  38.3 15.8 %all-gather = f32[1,1,6,4096]{2,3,1,0:T(8,128)S(1)} all-gather(f32[1,1,6,1024]{2,3,1,0:T(8,128)S(1)} %copy.51), channel_id=2, replica_groups=mesh['robot'=8,'sub'=4] {'sub'}, dimensions={3}, use_global_device_ids=true | all-gather | bytes 122880 | tf_op jit(solution)/shard_map/all_gather | solution.py:58
  54.1 1.0 copy.57
  55.1 2.8 %gather_fusion = f32[1024,6]{1,0:T(8,128)S(1)} fusion(f32[6,4096]{0,1:T(8,128)S(1)} %bitcast.55, s32[1024]{0:T(1024)S(1)} %broadcast_clamp_fusion.1), kind=kCustom, calls=%fused_computation | custom fusion | bytes 53248 | tf_op jit(solution)/shard_map/gather | solution.py:59
  58.0 0.0 copy-start.2
  58.0 22.9 %scatter_fusion = f32[6,1024]{0,1:T(8,128)S(1)} fusion(f32[6,1024]{0,1:T(8,128)S(1)} %bitcast.53, s32[4096]{0:T(1024)S(1)} %bitcast.67, f32[4096,6]{1,0:T(8,128)} %copy.55), kind=kCustom, calls=%fused_computation.3 | custom fusion | flops 24576 | bytes 311296 | tf_op jit(solution)/shard_map/vmap()/scatter-add | solution.py:66
  80.9 0.0 copy-start.8
  80.9 0.1 bitcast_subtract_fusion.1
  81.0 0.2 copy.58
  81.2 0.4 reduce
  81.6 0.0 copy-start.4
  81.6 0.0 copy-start.6
  81.6 0.1 multiply_reduce_fusion.1
  81.7 0.7 reshape.262
  82.4 0.1 copy.59
  82.6 0.0 all-to-all-done
  82.6 6.0 %all-to-all-start.1 = ((f32[8,1,256]{2,1,0:T(1,128)}), f32[8,1,256]{2,1,0:T(1,128)S(1)}, u32[]{:S(2)}, u32[]{:S(2)}) async-start(f32[8,1,256]{2,1,0:T(1,128)} %reshape.262), calls=%async_computation.1 | async-start | bytes 16384 | tf_op jit(solution)/shard_map/all_to_all | solution.py:38
  88.6 0.1 broadcast_in_dim_squeeze.8
  88.7 0.7 reduce.17
  89.3 0.1 reshape.227
  89.4 5.7 %all-to-all-done.1 = f32[8,1,256]{2,1,0:T(1,128)S(1)} async-done(((f32[8,1,256]{2,1,0:T(1,128)}), f32[8,1,256]{2,1,0:T(1,128)S(1)}, u32[]{:S(2)}, u32[]{:S(2)}) %all-to-all-start.1) | async-done | bytes 8224 | tf_op jit(solution)/shard_map/all_to_all | solution.py:38
  95.1 0.5 broadcast.117
  95.6 0.7 reduce.18
  96.3 0.1 reshape.263
  96.4 0.1 reshape.226
  96.5 0.1 copy.62
  96.6 2.3 %scatter_custom_fusion.1 = f32[4,512]{0,1:T(8,128)S(1)} fusion(s32[512]{0:T(512)S(1)} %reshape.227, f32[512,4]{1,0:T(8,128)S(1)} %copy.62, f32[]{:T(128)} %constant.10.clone.1), kind=kCustom, calls=%fused_computation.21 | custom fusion | flops 2048 | bytes 8196 | tf_op jit(solution)/shard_map/vmap()/scatter-add | solution.py:42
  98.9 0.3 slice_reduce_fusion
  99.2 0.8 fusion
  100.0 1.0 gather_fusion.2
  101.1 0.1 copy.63
  101.2 0.7 reshape.264
  101.9 3.3 %all-to-all-start.2 = ((f32[8,1,192]{2,1,0:T(1,128)}), f32[8,1,192]{2,1,0:T(1,128)S(1)}, u32[]{:S(2)}, u32[]{:S(2)}) async-start(f32[8,1,192]{2,1,0:T(1,128)} %reshape.264), calls=%async_computation.2 | async-start | bytes 16384 | tf_op jit(solution)/shard_map/all_to_all | solution.py:47
  105.3 0.6 reshape_add_fusion
  105.9 0.1 reshape.192
  106.0 0.7 copy.68
  107.3 4.4 %all-to-all-done.2 = f32[8,1,192]{2,1,0:T(1,128)S(1)} async-done(((f32[8,1,192]{2,1,0:T(1,128)}), f32[8,1,192]{2,1,0:T(1,128)S(1)}, u32[]{:S(2)}, u32[]{:S(2)}) %all-to-all-start.2) | async-done | bytes 6176 | tf_op jit(solution)/shard_map/all_to_all | solution.py:47
  111.7 0.7 reduce.19
  112.4 0.1 reshape.265
  112.5 0.2 copy.67
  112.6 0.1 all_to_all.28
  112.7 0.7 fusion.4
  113.5 0.6 copy.69
  114.1 6.6 %all-reduce.1 = (f32[]{:T(128)}, f32[]{:T(128)}) all-reduce(f32[]{:T(128)S(6)} %mul_shard_map.3, f32[]{:T(128)} %fusion.4), channel_id=1, replica_groups=mesh['robot'=8,'sub'=4] {'sub'}, use_global_device_ids=true, to_apply=%region_8.0 | all-reduce | flops 2 | bytes 16 | tf_op jit(solution)/shard_map/psum | solution.py:53
  120.7 18.3 %all-reduce = (f32[1]{0:T(128)}, f32[1]{0:T(128)}) all-reduce(f32[1]{0:T(128)} %bitcast.22, f32[1]{0:T(128)} %bitcast.21), channel_id=1, replica_groups=mesh['robot'=8,'sub'=4] {'robot'}, use_global_device_ids=true, to_apply=%region_9.0 | all-reduce | flops 2 | bytes 16 | tf_op jit(solution)/shard_map/psum | solution.py:53
  139.0 1.8 %fusion.10 = f32[2]{0:T(128)} fusion(f32[1]{0:T(128)} %get-tuple-element.22, f32[1]{0:T(128)} %get-tuple-element.23), kind=kLoop, calls=%fused_computation.41 | loop fusion | flops 4 | bytes 16 | tf_op jit(solution)/shard_map/sqrt | solution.py:55
  (28 shorter events, 0.2 us)
Async XLA Ops:
  3.2 79.4 %all-to-all-start = ((s32[1,8,64]{2,0,1:T(1,128)}), s32[1,8,64]{2,0,1:T(1,128)S(1)}, u32[]{:S(2)}, u32[]{:S(2)}) async-start(s32[1,8,64]{2,0,1:T(1,128)} %all_to_all.22), calls=%async_computation | async-start | bytes 8192 | tf_op jit(solution)/shard_map/all_to_all | solution.py:39
  33.0 2.3 %copy-start.1 = (f32[1,1,18,4096]{3,1,2,0:T(1,128)S(1)}, f32[1,1,18,4096]{3,1,2,0:T(1,128)}, u32[]{:S(2)}) copy-start(f32[1,1,18,4096]{3,1,2,0:T(1,128)} %param.20) | copy-start | bytes 884740
  35.2 2.8 %copy-start.3 = (f32[1,1,6,1024]{3,1,2,0:T(1,128)S(1)}, f32[1,1,6,1024]{3,1,2,0:T(1,128)}, u32[]{:S(2)}) copy-start(f32[1,1,6,1024]{3,1,2,0:T(1,128)} %param.18) | copy-start | bytes 73732
  38.1 16.0 %copy-start.9 = (s32[1,1,1024]{2,1,0:T(1,128)S(1)}, s32[1,1,1024]{2,1,0:T(1,128)}, u32[]{:S(2)}) copy-start(s32[1,1,1024]{2,1,0:T(1,128)} %param.24) | copy-start | bytes 12292
  38.1 16.0 %copy-start.5 = (f32[1,1,6,1024]{3,1,2,0:T(1,128)S(1)}, f32[1,1,6,1024]{3,1,2,0:T(1,128)}, u32[]{:S(2)}) copy-start(f32[1,1,6,1024]{3,1,2,0:T(1,128)} %param.25) | copy-start | bytes 73732
  38.1 19.9 %copy-start.7 = (s32[1,1,4096]{2,1,0:T(1,128)S(1)}, s32[1,1,4096]{2,1,0:T(1,128)}, u32[]{:S(2)}) copy-start(s32[1,1,4096]{2,1,0:T(1,128)} %param.22) | copy-start | bytes 49156
  57.9 23.0 %copy-start = (f32[1,1,6,1024]{2,3,1,0:T(8,128)S(1)}, f32[1,1,6,1024]{2,3,1,0:T(8,128)}, u32[]{:S(2)}) copy-start(f32[1,1,6,1024]{2,3,1,0:T(8,128)} %copy.57) | copy-start | bytes 73732
  58.0 23.2 %copy-start.2 = (f32[1,1,36,1024]{3,1,2,0:T(1,128)S(1)}, f32[1,1,36,1024]{3,1,2,0:T(1,128)}, u32[]{:S(2)}) copy-start(f32[1,1,36,1024]{3,1,2,0:T(1,128)} %param.19) | copy-start | bytes 442372
  80.9 1.5 %copy-start.8 = (f32[1,1,3,512]{3,1,2,0:T(1,128)S(1)}, f32[1,1,3,512]{3,1,2,0:T(1,128)}, u32[]{:S(2)}) copy-start(f32[1,1,3,512]{3,1,2,0:T(1,128)} %param.17) | copy-start | bytes 18436
  81.6 31.9 %copy-start.4 = (f32[1,1,3,512]{3,1,2,0:T(1,128)S(1)}, f32[1,1,3,512]{3,1,2,0:T(1,128)}, u32[]{:S(2)}) copy-start(f32[1,1,3,512]{3,1,2,0:T(1,128)} %param.13) | copy-start | bytes 18436
  81.6 31.9 %copy-start.6 = (f32[1,1,3,512]{3,1,2,0:T(1,128)S(1)}, f32[1,1,3,512]{3,1,2,0:T(1,128)}, u32[]{:S(2)}) copy-start(f32[1,1,3,512]{3,1,2,0:T(1,128)} %param.14) | copy-start | bytes 18436
  82.6 12.5 %all-to-all-start.1 = ((f32[8,1,256]{2,1,0:T(1,128)}), f32[8,1,256]{2,1,0:T(1,128)S(1)}, u32[]{:S(2)}, u32[]{:S(2)}) async-start(f32[8,1,256]{2,1,0:T(1,128)} %reshape.262), calls=%async_computation.1 | async-start | bytes 16384 | tf_op jit(solution)/shard_map/all_to_all | solution.py:38
  101.9 9.8 %all-to-all-start.2 = ((f32[8,1,192]{2,1,0:T(1,128)}), f32[8,1,192]{2,1,0:T(1,128)S(1)}, u32[]{:S(2)}, u32[]{:S(2)}) async-start(f32[8,1,192]{2,1,0:T(1,128)} %reshape.264), calls=%async_computation.2 | async-start | bytes 16384 | tf_op jit(solution)/shard_map/all_to_all | solution.py:47
